TPU v7x, 32 devices: a whole 2x2x4 slice. The times are simulated.
32 devices in a mesh: batch: 2 (over y), space: 8 (over z, x), hidden: 2 (over core).
Axes of the slice: x: 2, y: 2, z: 4, core: 2. Of those that a mesh axis runs over, the one named last changes fastest.
Arguments:
- nodes: bfloat16 [2, 1024, 512], P('batch', 'space'), may hold values from -6 to 6
- edges: bfloat16 [2, 8192, 512], P('batch', 'space'), may hold values from -6 to 6
- node_cotangent: bfloat16 [2, 1024, 512], P('batch', 'space'), may hold values from -18 to 18
- edge_cotangent: bfloat16 [2, 8192, 512], P('batch', 'space'), may hold values from -18 to 18
- senders: int32 [8192], P('space'), may hold values from 0 to 255
- receivers: int32 [8192], P('space'), may hold values from 0 to 127
- send_lists: int32 [8, 2, 64], P('space'), may hold values from 0 to 127
- edge_first: bfloat16 [1536, 512], P(None, 'hidden'), may hold values from -0.15625 to 0.15625
- edge_bias: float32 [512], P('hidden'), may hold values from -3 to 3
- edge_second: bfloat16 [512, 512], P('hidden'), may hold values from -0.25 to 0.25
- edge_gain: float32 [512], replicated, may hold values from 0.1 to 1.9
- node_first: bfloat16 [1024, 512], replicated, may hold values from -0.1875 to 0.1875
- node_bias: float32 [512], replicated, may hold values from -3 to 3
- node_second: bfloat16 [512, 512], replicated, may hold values from -0.25 to 0.25
- node_gain: float32 [512], replicated, may hold values from 0.1 to 1.9
Outputs:
- grad_nodes: bfloat16 [2, 1024, 512], P('batch', 'space', 'hidden')
- grad_edges: bfloat16 [2, 8192, 512], P('batch', 'space', 'hidden')
- grad_edge_first: float32 [1536, 512], P(None, 'hidden')
- grad_edge_bias: float32 [512], P('hidden')
- grad_edge_second: float32 [512, 512], P('hidden')
- grad_edge_gain: float32 [512], replicated
- grad_node_first: float32 [1024, 512], replicated
- grad_node_bias: float32 [512], replicated
- grad_node_second: float32 [512, 512], replicated
- grad_node_gain: float32 [512], replicated
Inputs may be any that keep to these rules, and one draw needn't show every extreme that they name: `senders`: an entry below 128 is a local node of the edge's patch; 128 + k is row k of the previous patch's list 1, 192 + k row k of the next patch's list 0. `receivers`: local nodes of the edge's patch. `send_lists`: local nodes of the patch; entries may repeat.
All inputs are finite; a program needn't handle non-finite values.
Results may differ from a plain program's by a relative error of at most 0.015.
Values may be sent and summed in bfloat16 or wider, within the bound.
A program may use at most 128 MiB of HBM per device.

v0:
```python
import jax
import jax.numpy as jnp
from jax import lax
from jax.sharding import PartitionSpec as P

EPS = 1e-05


def extended(cells, sides, width):
    for axis, dim in sides:
        count = lax.axis_size(axis)
        head = lax.slice_in_dim(cells, 0, width, axis=dim)
        tail = lax.slice_in_dim(cells, cells.shape[dim] - width, cells.shape[dim], axis=dim)
        cells = jnp.concatenate(
            [
                lax.ppermute(tail, axis, [(i, (i + 1) % count) for i in range(count)]),
                cells,
                lax.ppermute(head, axis, [((i + 1) % count, i) for i in range(count)]),
            ],
            axis=dim,
        )
    return cells


def one_hot(indices, columns, wanted):
    return (indices[:, None] == jnp.arange(columns, dtype=jnp.int32)[None, :]).astype(wanted)


def matmul(lefthand, righthand):
    return jnp.dot(lefthand, righthand, preferred_element_type=jnp.float32)


def matmul_tn(lefthand, righthand):
    return lax.dot_general(
        lefthand, righthand, (((0,), (0,)), ((), ())), preferred_element_type=jnp.float32
    )


def matmul_nt(lefthand, righthand):
    return lax.dot_general(
        lefthand, righthand, (((1,), (1,)), ((), ())), preferred_element_type=jnp.float32
    )


def exact_tn(lefthand, righthand):
    return lax.dot_general(
        lefthand,
        righthand,
        (((0,), (0,)), ((), ())),
        precision=lax.Precision.HIGHEST,
        preferred_element_type=jnp.float32,
    )


def normalize(values):
    centre = values - jnp.mean(values, axis=-1, keepdims=True)
    scaled = lax.rsqrt(jnp.mean(centre * centre, axis=-1, keepdims=True) + EPS)
    return (centre * scaled, scaled)


def norm_back(upstream, gain_vec, normed, scaled):
    pulled = upstream * gain_vec
    return scaled * (
        pulled
        - jnp.mean(pulled, axis=-1, keepdims=True)
        - normed * jnp.mean(pulled * normed, axis=-1, keepdims=True)
    )


def silu_slope(values):
    logistic = jax.nn.sigmoid(values)
    return logistic * (1.0 + values * (1.0 - logistic))


def on_device(
    nodes,
    edges,
    node_cotangent,
    edge_cotangent,
    senders,
    receivers,
    send_lists,
    edge_first,
    edge_bias,
    edge_second,
    edge_gain,
    node_first,
    node_bias,
    node_second,
    node_gain,
):
    splits = lax.axis_size("hidden")
    my_part = lax.axis_index("hidden")
    width = nodes.shape[2]
    half = width // splits
    node_rows = nodes[0]
    node_count = node_rows.shape[0]
    halo_count = send_lists.shape[2]
    listed = send_lists[0].reshape(-1)
    picker = one_hot(listed, node_count, jnp.bfloat16)
    outgoing = matmul(picker, node_rows).astype(jnp.bfloat16).reshape(2, halo_count, width)
    padded = extended(outgoing, (("space", 0),), 1)
    table = jnp.concatenate([node_rows, padded[0], padded[3]], axis=0)
    table_rows = table.shape[0]
    sender_hot = one_hot(senders, table_rows, jnp.bfloat16)
    receiver_hot = one_hot(receivers, node_count, jnp.bfloat16)
    from_sender = matmul(sender_hot, table).astype(jnp.bfloat16)
    from_receiver = matmul(receiver_hot, node_rows).astype(jnp.bfloat16)
    edge_input = jnp.concatenate([edges[0], from_sender, from_receiver], axis=1)
    edge_pre = matmul(edge_input, edge_first) + edge_bias
    edge_act = jax.nn.silu(edge_pre).astype(jnp.bfloat16)
    edge_total = lax.psum(matmul(edge_act, edge_second).astype(jnp.bfloat16), "hidden").astype(
        jnp.float32
    )
    edge_normed, edge_scale = normalize(edge_total)
    message = (edge_gain * edge_normed).astype(jnp.bfloat16)
    gathered = matmul_tn(receiver_hot, message).astype(jnp.bfloat16)
    node_input = jnp.concatenate([node_rows, gathered], axis=1)
    node_pre = matmul(node_input, node_first) + node_bias
    node_act = jax.nn.silu(node_pre).astype(jnp.bfloat16)
    node_normed, node_scale = normalize(matmul(node_act, node_second))
    node_upstream = node_cotangent[0].astype(jnp.float32)
    node_gain_grad = jnp.sum(node_upstream * node_normed, axis=0)
    node_dz = norm_back(node_upstream, node_gain, node_normed, node_scale).astype(jnp.bfloat16)
    node_second_grad = matmul_tn(node_act, node_dz)
    node_dh = (matmul_nt(node_dz, node_second) * silu_slope(node_pre)).astype(jnp.bfloat16)
    node_first_grad = matmul_tn(node_input, node_dh)
    node_bias_grad = jnp.sum(node_dh.astype(jnp.float32), axis=0)
    node_dx = matmul_nt(node_dh, node_first)
    agg_grad = node_dx[:, width:].astype(jnp.bfloat16)
    edge_upstream = edge_cotangent[0].astype(jnp.float32)
    message_grad = edge_upstream + matmul(receiver_hot, agg_grad)
    edge_gain_grad = jnp.sum(message_grad * edge_normed, axis=0)
    edge_dz = norm_back(message_grad, edge_gain, edge_normed, edge_scale).astype(jnp.bfloat16)
    edge_second_grad = matmul_tn(edge_act, edge_dz)
    edge_dh = (matmul_nt(edge_dz, edge_second) * silu_slope(edge_pre)).astype(jnp.bfloat16)
    edge_first_grad = matmul_tn(edge_input, edge_dh)
    edge_bias_grad = jnp.sum(edge_dh.astype(jnp.float32), axis=0)
    sender_exact = one_hot(senders, table_rows, jnp.float32)
    receiver_exact = one_hot(receivers, node_count, jnp.float32)
    blocks = edge_first.reshape(3, splits, half, edge_first.shape[1])
    mine = lax.all_to_all(blocks, "hidden", split_axis=1, concat_axis=3, tiled=True).reshape(
        3 * half, -1
    )
    input_grad = matmul_nt(lax.all_gather(edge_dh, "hidden", axis=1, tiled=True), mine)
    edge_own = input_grad[:, :half]
    sender_grad = exact_tn(sender_exact, input_grad[:, half : 2 * half])
    receiver_grad = exact_tn(receiver_exact, input_grad[:, 2 * half :])
    table_grad = jnp.concatenate(
        [sender_grad[:node_count] + receiver_grad, sender_grad[node_count:]], axis=0
    )
    returning = jnp.stack(
        [table_grad[node_count : node_count + halo_count], table_grad[node_count + halo_count :]],
        axis=0,
    )
    returned = extended(returning.astype(jnp.bfloat16), (("space", 0),), 1).astype(returning.dtype)
    arriving = jnp.concatenate([returned[0], returned[3]], axis=0)
    halo_grad = exact_tn(one_hot(listed, node_count, jnp.float32), arriving)
    own_cot = lax.dynamic_slice_in_dim(node_upstream, my_part * half, half, 1)
    own_node = lax.dynamic_slice_in_dim(node_dx, my_part * half, half, 1)
    grad_nodes = (own_cot + own_node + table_grad[:node_count] + halo_grad).astype(jnp.bfloat16)[
        None
    ]
    own_edge_cot = lax.dynamic_slice_in_dim(edge_upstream, my_part * half, half, 1)
    grad_edges = (own_edge_cot + edge_own).astype(jnp.bfloat16)[None]
    (
        edge_first_grad,
        edge_bias_grad,
        edge_second_grad,
        edge_gain_grad,
        node_first_grad,
        node_bias_grad,
        node_second_grad,
        node_gain_grad,
    ) = lax.psum(
        (
            edge_first_grad,
            edge_bias_grad,
            edge_second_grad,
            edge_gain_grad,
            node_first_grad,
            node_bias_grad,
            node_second_grad,
            node_gain_grad,
        ),
        ("batch", "space"),
    )
    return (
        grad_nodes,
        grad_edges,
        edge_first_grad,
        edge_bias_grad,
        edge_second_grad,
        edge_gain_grad,
        node_first_grad,
        node_bias_grad,
        node_second_grad,
        node_gain_grad,
    )


def solution(mesh):
    placed = (
        P("batch", "space", None),
        P("batch", "space", None),
        P("batch", "space", None),
        P("batch", "space", None),
        P("space"),
        P("space"),
        P("space", None, None),
        P(None, "hidden"),
        P("hidden"),
        P("hidden", None),
        P(),
        P(),
        P(),
        P(),
        P(),
    )
    return jax.shard_map(
        on_device,
        mesh=mesh,
        in_specs=placed,
        out_specs=(
            P("batch", "space", "hidden"),
            P("batch", "space", "hidden"),
            P(None, "hidden"),
            P("hidden"),
            P("hidden", None),
            P(),
            P(),
            P(),
            P(),
            P(),
        ),
        check_vma=False,
    )
```

profile of v0, /device:TPU:0, one launch (start us, length us, event | category | flops | bytes accessed | tf_op | source)
XLA Modules:
  0.0 280.4 jit_solution(7566066074686124205)
XLA Ops:
  8.7 1.1 convolution_convert_fusion.4
  9.8 3.0 %collective-permute-start = (bf16[1,64,512]{2,1,0:T(8,128)(2,1)S(1)}, bf16[1,64,512]{2,1,0:T(8,128)(2,1)S(1)}, u32[]{:S(2)}, u32[]{:S(2)}) collective-permute-start(bf16[1,64,512]{2,1,0:T(8,128)(2,1)S(1)} %get-tuple-element.28), channel_id=1, source_target_pairs={{0,2},{2,4},{4,6},{6,8},{8,10},{10,12},{12,14},{14,0},{1,3},{3,5},... | collective-permute-start | bytes 196616 | tf_op jit(solution)/shard_map/ppermute | solution.py:16
  12.9 3.1 %collective-permute-start.1 = (bf16[1,64,512]{2,1,0:T(8,128)(2,1)S(1)}, bf16[1,64,512]{2,1,0:T(8,128)(2,1)S(1)}, u32[]{:S(2)}, u32[]{:S(2)}) collective-permute-start(bf16[1,64,512]{2,1,0:T(8,128)(2,1)S(1)} %get-tuple-element.29), channel_id=1, source_target_pairs={{2,0},{4,2},{6,4},{8,6},{10,8},{12,10},{14,12},{0,14},{3,1},{5,3},... | collective-permute-start | bytes 196616 | tf_op jit(solution)/shard_map/ppermute | solution.py:18
  16.0 1.5 convolution_convert_fusion.2
  17.5 1.3 copy.33
  19.4 2.9 %convolution_add_fusion = f32[1024,256]{1,0:T(8,128)S(1)} fusion(bf16[1536,256]{1,0:T(8,128)(2,1)} %param.22, bf16[1024,512]{0,1:T(8,128)(2,1)S(1)} %convolution_convert_fusion.2, bf16[1024,512]{0,1:T(8,128)(2,1)S(1)} %convolution_convert_fusion, bf16[1024,512]{0,1:T(8,128)(2,1)} %bitcast.76, f32[256]{0:T(256)S(1)} %copy-done.35), kind=kOutput, calls=%fused_computation.22 | convolution fusion | flops 815005696 | bytes 4981760 | tf_op jit(solution)/shard_map/dot_general | solution.py:30
  22.3 1.4 convolution_convert_fusion.1
  23.8 20.5 %all-reduce.5.cloned.1.call-done = bf16[1024,512]{1,0:T(8,128)(2,1)} async-done(((bf16[1024,512]{1,0:T(8,128)(2,1)}), bf16[1024,512]{1,0:T(8,128)(2,1)}) %all-reduce.5.cloned.1.call-update) | async-done | bytes 1048592 | tf_op jit(solution)/shard_map/psum | solution.py:112
  44.4 1.5 convert_reduce_fusion
  45.9 1.7 fusion.12
  51.9 1.9 fusion.11
  55.1 1.9 convert_reduce_fusion.1
  57.1 2.5 fusion.55
  59.6 2.7 fusion.41
  62.4 1.3 fusion.57
  64.3 2.1 fusion.14
  66.4 1.1 copy-done.9
  68.5 4.4 %all-to-all-start = ((bf16[3,2,256,256]{3,2,0,1:T(8,128)(2,1)}), bf16[3,2,256,256]{3,2,0,1:T(8,128)(2,1)}, u32[]{:S(2)}, u32[]{:S(2)}) async-start(bf16[3,2,256,256]{3,2,0,1:T(8,128)(2,1)} %copy.35), calls=%async_computation | async-start | bytes 1572864 | tf_op jit(solution)/shard_map/all_to_all | solution.py:142
  72.9 1.5 convert_element_type.87
  75.0 1.9 copy.36
  76.9 1.1 copy.38
  78.0 46.1 %all-reduce = (f32[256]{0:T(256)}, f32[512]{0:T(512)}, f32[512]{0:T(512)}, f32[512]{0:T(512)}) all-reduce(f32[256]{0:T(256)S(1)} %copy-done.28, f32[512]{0:T(512)S(1)} %copy-done.27, f32[512]{0:T(512)S(1)} %copy-done.26, f32[512]{0:T(512)S(1)} %get-tuple-element.13), channel_id=1, replica_groups=mesh['batch'=2,'space'=8,'hidden'=2] {'batch','space'}, use_global_device_ids=true, to_apply=%region_11.12 | all-reduce | flops 1792 | bytes 14336 | tf_op jit(solution)/shard_map/psum | solution.py:175
  124.1 2.5 fusion.61
  126.6 1.2 fusion.59
  127.9 4.7 %collective-permute-start.3 = (bf16[1,64,256]{2,1,0:T(8,128)(2,1)S(1)}, bf16[1,64,256]{2,1,0:T(8,128)(2,1)S(1)}, u32[]{:S(2)}, u32[]{:S(2)}) collective-permute-start(bf16[1,64,256]{2,1,0:T(8,128)(2,1)S(1)} %get-tuple-element.27), channel_id=1, source_target_pairs={{2,0},{4,2},{6,4},{8,6},{10,8},{12,10},{14,12},{0,14},{3,1},{5,3},... | collective-permute-start | bytes 98312 | tf_op jit(solution)/shard_map/ppermute | solution.py:18
  132.6 1.0 fusion.27
  133.5 1.7 fusion.16
  135.3 1.0 fusion.18
  136.3 131.0 %all-reduce.7.cloned.1.call-done = (f32[1536,256]{1,0:T(8,128)}, f32[256,512]{1,0:T(8,128)}, f32[1024,512]{1,0:T(8,128)}, f32[512,512]{1,0:T(8,128)}) async-done(((f32[1536,256]{1,0:T(8,128)}, f32[256,512]{1,0:T(8,128)}, f32[1024,512]{1,0:T(8,128)}, f32[512,512]{1,0:T(8,128)}), (f32[1536,256]{1,0:T(8,128)}, f32[256,512]{1,0:T(8,128)}, f32[1024,512]{1,0:T(8,128)}, ...) | async-done | bytes 5242896 | tf_op jit(solution)/shard_map/psum | solution.py:175
  267.3 2.8 copy.44
  270.9 1.3 copy.46
  272.9 1.0 copy.47
  (117 shorter events, 11.2 us)
Async XLA Ops:
  7.2 41.4 %copy-start = (bf16[1024,512]{1,0:T(8,128)(2,1)S(1)}, bf16[1024,512]{1,0:T(8,128)(2,1)}, u32[]{:S(2)}) copy-start(bf16[1024,512]{1,0:T(8,128)(2,1)} %param.26) | copy-start | bytes 3145732
  7.2 11.6 %copy-start.2 = (bf16[1,128,512]{2,1,0:T(8,128)(2,1)S(1)}, bf16[1,128,512]{2,1,0:T(8,128)(2,1)}, u32[]{:S(2)}) copy-start(bf16[1,128,512]{2,1,0:T(8,128)(2,1)} %param.15) | copy-start | bytes 393220
  7.2 10.2 %copy-start.5 = (bf16[1,1024,512]{2,1,0:T(8,128)(2,1)S(1)}, bf16[1,1024,512]{2,1,0:T(8,128)(2,1)}, u32[]{:S(2)}) copy-start(bf16[1,1024,512]{2,1,0:T(8,128)(2,1)} %param.16) | copy-start | bytes 3145732
  7.2 11.6 %copy-start.18 = (s32[1024]{0:T(1024)S(1)}, s32[1024]{0:T(1024)}, u32[]{:S(2)}) copy-start(s32[1024]{0:T(1024)} %param.19) | copy-start | bytes 12292
  7.2 37.1 %all-reduce.5.cloned.1.call-start = ((), (), s32[]{:S(2)}) async-start(), calls=%async_computation.1 | async-start | bytes 2097152 | tf_op jit(solution)/shard_map/psum | solution.py:112
  9.8 8.9 %collective-permute-start = (bf16[1,64,512]{2,1,0:T(8,128)(2,1)S(1)}, bf16[1,64,512]{2,1,0:T(8,128)(2,1)S(1)}, u32[]{:S(2)}, u32[]{:S(2)}) collective-permute-start(bf16[1,64,512]{2,1,0:T(8,128)(2,1)S(1)} %get-tuple-element.28), channel_id=1, source_target_pairs={{0,2},{2,4},{4,6},{6,8},{8,10},{10,12},{12,14},{14,0},{1,3},{3,5},... | collective-permute-start | bytes 196616 | tf_op jit(solution)/shard_map/ppermute | solution.py:16
  12.9 5.9 %collective-permute-start.1 = (bf16[1,64,512]{2,1,0:T(8,128)(2,1)S(1)}, bf16[1,64,512]{2,1,0:T(8,128)(2,1)S(1)}, u32[]{:S(2)}, u32[]{:S(2)}) collective-permute-start(bf16[1,64,512]{2,1,0:T(8,128)(2,1)S(1)} %get-tuple-element.29), channel_id=1, source_target_pairs={{2,0},{4,2},{6,4},{8,6},{10,8},{12,10},{14,12},{0,14},{3,1},{5,3},... | collective-permute-start | bytes 196616 | tf_op jit(solution)/shard_map/ppermute | solution.py:18
  19.4 2.9 %copy-start.36 = (bf16[1024,512]{0,1:T(8,128)(2,1)}, bf16[1024,512]{0,1:T(8,128)(2,1)S(1)}, u32[]{:S(2)}) copy-start(bf16[1024,512]{0,1:T(8,128)(2,1)S(1)} %convolution_convert_fusion) | copy-start | bytes 3145732
  19.4 2.9 %copy-start.33 = (bf16[256,512]{1,0:T(8,128)(2,1)S(1)}, bf16[256,512]{1,0:T(8,128)(2,1)}, u32[]{:S(2)}) copy-start(bf16[256,512]{1,0:T(8,128)(2,1)} %param.24) | copy-start | bytes 786436
  23.8 23.8 %copy-start.17 = (s32[1024]{0:T(1024)S(1)}, s32[1024]{0:T(1024)}, u32[]{:S(2)}) copy-start(s32[1024]{0:T(1024)} %param.20) | copy-start | bytes 12292
  23.8 23.8 %copy-start.20 = (f32[512]{0:T(512)S(1)}, f32[512]{0:T(512)}, u32[]{:S(2)}) copy-start(f32[512]{0:T(512)} %param.25) | copy-start | bytes 6148
  23.8 100.3 %all-gather.2.cloned.1.call-start = ((), (), s32[]{:S(2)}) async-start(), calls=%async_computation.2 | async-start | bytes 1572864 | tf_op jit(solution)/shard_map/all_gather | solution.py:145
  44.3 3.3 %copy-start.1 = (bf16[1024,512]{1,0:T(8,128)(2,1)S(1)}, bf16[1024,512]{1,0:T(8,128)(2,1)}, u32[]{:S(2)}) copy-start(bf16[1024,512]{1,0:T(8,128)(2,1)} %all-reduce.5.cloned.1.call-done) | copy-start | bytes 3145732
  45.9 2.7 copy-start.19
  48.5 2.2 copy-start.12
  49.5 2.3 copy-start.29
  49.8 2.1 copy-start.4
  49.8 4.0 %copy-start.30 = (f32[128]{0:T(128)}, f32[128]{0:T(128)S(1)}, u32[]{:S(2)}) copy-start(f32[128]{0:T(128)S(1)} %get-tuple-element.39) | copy-start | bytes 1540
  49.8 3.9 %copy-start.31 = (f32[128]{0:T(128)}, f32[128]{0:T(128)S(1)}, u32[]{:S(2)}) copy-start(f32[128]{0:T(128)S(1)} %get-tuple-element.40) | copy-start | bytes 1540
  55.1 2.0 copy-start.22
  57.0 210.2 %all-reduce.7.cloned.1.call-start = ((), (), s32[]{:S(2)}) async-start(), calls=%async_computation.3 | async-start | bytes 10485760 | tf_op jit(solution)/shard_map/psum | solution.py:175
  57.1 5.3 %copy-start.40 = (f32[1024,256]{1,0:T(8,128)S(1)}, f32[1024,256]{1,0:T(8,128)}, u32[]{:S(2)}) copy-start(f32[1024,256]{1,0:T(8,128)} %copy-done.38) | copy-start | bytes 3145732
  68.5 6.0 %copy-start.11 = (bf16[1,128,512]{2,1,0:T(8,128)(2,1)S(1)}, bf16[1,128,512]{2,1,0:T(8,128)(2,1)}, u32[]{:S(2)}) copy-start(bf16[1,128,512]{2,1,0:T(8,128)(2,1)} %param.17) | copy-start | bytes 393220
  68.5 6.5 %all-to-all-start = ((bf16[3,2,256,256]{3,2,0,1:T(8,128)(2,1)}), bf16[3,2,256,256]{3,2,0,1:T(8,128)(2,1)}, u32[]{:S(2)}, u32[]{:S(2)}) async-start(bf16[3,2,256,256]{3,2,0,1:T(8,128)(2,1)} %copy.35), calls=%async_computation | async-start | bytes 1572864 | tf_op jit(solution)/shard_map/all_to_all | solution.py:142
  74.5 3.5 %copy-start.26 = (f32[512]{0:T(512)S(1)}, f32[512]{0:T(512)}, u32[]{:S(2)}) copy-start(f32[512]{0:T(512)} %get-tuple-element.37) | copy-start | bytes 6148
  74.5 3.5 %copy-start.27 = (f32[512]{0:T(512)S(1)}, f32[512]{0:T(512)}, u32[]{:S(2)}) copy-start(f32[512]{0:T(512)} %get-tuple-element.10) | copy-start | bytes 6148
  74.5 3.5 %copy-start.28 = (f32[256]{0:T(256)S(1)}, f32[256]{0:T(256)}, u32[]{:S(2)}) copy-start(f32[256]{0:T(256)} %get-tuple-element.35) | copy-start | bytes 3076
  127.8 7.5 %collective-permute-start.2 = (bf16[1,64,256]{2,1,0:T(8,128)(2,1)S(1)}, bf16[1,64,256]{2,1,0:T(8,128)(2,1)S(1)}, u32[]{:S(2)}, u32[]{:S(2)}) collective-permute-start(bf16[1,64,256]{2,1,0:T(8,128)(2,1)S(1)} %get-tuple-element.26), channel_id=1, source_target_pairs={{0,2},{2,4},{4,6},{6,8},{8,10},{10,12},{12,14},{14,0},{1,3},{3,5},... | collective-permute-start | bytes 98312 | tf_op jit(solution)/shard_map/ppermute | solution.py:16
  127.9 7.4 %copy-start.24 = (s32[128]{0:T(128)S(1)}, s32[128]{0:T(128)}, u32[]{:S(2)}) copy-start(s32[128]{0:T(128)} %copy-done.23) | copy-start | bytes 1540
  127.9 7.4 %collective-permute-start.3 = (bf16[1,64,256]{2,1,0:T(8,128)(2,1)S(1)}, bf16[1,64,256]{2,1,0:T(8,128)(2,1)S(1)}, u32[]{:S(2)}, u32[]{:S(2)}) collective-permute-start(bf16[1,64,256]{2,1,0:T(8,128)(2,1)S(1)} %get-tuple-element.27), channel_id=1, source_target_pairs={{2,0},{4,2},{6,4},{8,6},{10,8},{12,10},{14,12},{0,14},{3,1},{5,3},... | collective-permute-start | bytes 98312 | tf_op jit(solution)/shard_map/ppermute | solution.py:18
  267.3 2.8 %copy-start.13 = (f32[256,512]{1,0:T(8,128)S(1)}, f32[256,512]{1,0:T(8,128)}, u32[]{:S(2)}) copy-start(f32[256,512]{1,0:T(8,128)} %get-tuple-element.45) | copy-start | bytes 1572868
  267.3 3.6 %copy-start.3 = (f32[1024,512]{1,0:T(8,128)S(1)}, f32[1024,512]{1,0:T(8,128)}, u32[]{:S(2)}) copy-start(f32[1024,512]{1,0:T(8,128)} %get-tuple-element.47) | copy-start | bytes 6291460
  (17 other events, 22.9 us)
Sparse Core Ops, SparseCore 0:
  23.9 20.3 all-reduce.4
  57.2 9.9 all-gather.1
  73.9 193.3 all-reduce.6
where the time goes:
time: 281 us; the launch traced here: 280 us
  waiting for transfers between devices  152 us (54%)
  blocking collectives  46.1 us (16%)
  matrix products  29.2 us (10%)
  local copies, waits for them, and re-layouts  16.2 us (6%)
  starting transfers between devices  15.4 us (5%)
  between operations  14.3 us (5%)
  other arithmetic  7.05 us (3%)
    psum x1, waiting for transfers between devices, on_device(): lax.psum((edge_first_grad, edge_bias_grad, edge_second_grad, edge_gain_gr...  131 us
    psum x1, blocking collectives, on_device(): lax.psum((edge_first_grad, edge_bias_grad, edge_second_grad, edge_gain_gr...  46.1 us
    psum x1, waiting for transfers between devices, on_device(): lax.psum(matmul(edge_act, edge_second).astype(jnp.bfloat16), 'hidden')  20.5 us
    unnamed x88, local copies, waits for them, and re-layouts  12.4 us
    dot_general x8, matrix products, matmul(): return jnp.dot(lefthand, righthand, preferred_element_type=jnp.float32)  9.97 us
    dot_general x5, matrix products, matmul_tn(): lax.dot_general(lefthand, righthand, (((0,), (0,)), ((), ())), preferred_...  9.58 us
    ppermute x2, starting transfers between devices, extended(): lax.ppermute(head, axis, [((i + 1) % count, i) for i in range(count)])  7.8 us
    dot_general x4, matrix products, matmul_nt(): lax.dot_general(lefthand, righthand, (((1,), (1,)), ((), ())), preferred_...  5.78 us
  transfers between devices with their start and end apart: 8, of which 3 were waited for; matrix products, arithmetic and copies ran while one was open for 9% of the time, Pallas kernels for 0%

commit v1 on v0

--- a/solution.py
+++ b/solution.py
@@ -173,17 +173,20 @@
         node_second_grad,
         node_gain_grad,
     ) = lax.psum(
-        (
-            edge_first_grad,
-            edge_bias_grad,
-            edge_second_grad,
-            edge_gain_grad,
-            node_first_grad,
-            node_bias_grad,
-            node_second_grad,
-            node_gain_grad,
+        lax.psum(
+            (
+                edge_first_grad,
+                edge_bias_grad,
+                edge_second_grad,
+                edge_gain_grad,
+                node_first_grad,
+                node_bias_grad,
+                node_second_grad,
+                node_gain_grad,
+            ),
+            "space",
         ),
-        ("batch", "space"),
+        "batch",
     )
     return (
         grad_nodes,

time: 281 us -> 408 us (1.45)
  waiting for transfers between devices: 152 us -> 301 us
  blocking collectives: 46.1 us -> 25.5 us
    psum x0 -> x1, waiting for transfers between devices: none -> 95.3 us  [on_device(): lax.psum(lax.psum((edge_first_grad, edge_bias_grad, edge_second_grad, edg...]
    psum x1, waiting for transfers between devices: 131 us -> 184 us  [on_device(): lax.psum((edge_first_grad, edge_bias_grad, edge_second_grad, edge_gain_gr...]
    psum x1, blocking collectives: 46.1 us -> 19.4 us  [on_device(): lax.psum((edge_first_grad, edge_bias_grad, edge_second_grad, edge_gain_gr...]
    psum x0 -> x1, blocking collectives: none -> 6.05 us  [on_device(): lax.psum(lax.psum((edge_first_grad, edge_bias_grad, edge_second_grad, edg...]
    unnamed x88 -> x58, local copies, waits for them, and re-layouts: 12.4 us -> 11.4 us
  transfers between devices with their start and end apart: 8 -> 9, of which waited for: 3 -> 4; matrix products, arithmetic and copies ran while one was open for 9% -> 4% of each run, Pallas kernels for 0% -> 0%
where the time goes in v1:
time: 408 us; the launch traced here: 407 us
  waiting for transfers between devices  301 us (74%)
  matrix products  28.5 us (7%)
  blocking collectives  25.5 us (6%)
  starting transfers between devices  15.4 us (4%)
  local copies, waits for them, and re-layouts  15.3 us (4%)
  between operations  14.2 us (3%)
  other arithmetic  7.11 us (2%)
    psum x1, waiting for transfers between devices, on_device(): lax.psum((edge_first_grad, edge_bias_grad, edge_second_grad, edge_gain_gr...  184 us
    psum x1, waiting for transfers between devices, on_device(): lax.psum(lax.psum((edge_first_grad, edge_bias_grad, edge_second_grad, edg...  95.3 us
    psum x1, waiting for transfers between devices, on_device(): lax.psum(matmul(edge_act, edge_second).astype(jnp.bfloat16), 'hidden')  20.5 us
    psum x1, blocking collectives, on_device(): lax.psum((edge_first_grad, edge_bias_grad, edge_second_grad, edge_gain_gr...  19.4 us
    unnamed x58, local copies, waits for them, and re-layouts  11.4 us
    dot_general x8, matrix products, matmul(): return jnp.dot(lefthand, righthand, preferred_element_type=jnp.float32)  9.99 us
    dot_general x5, matrix products, matmul_tn(): lax.dot_general(lefthand, righthand, (((0,), (0,)), ((), ())), preferred_...  8.89 us
  transfers between devices with their start and end apart: 9, of which 4 were waited for; matrix products, arithmetic and copies ran while one was open for 4% of the time, Pallas kernels for 0%

profile of v1, /device:TPU:0, one launch (start us, length us, event | category | flops | bytes accessed | tf_op | source)
XLA Modules:
  0.0 407.4 jit_solution(2829657583601995586)
XLA Ops:
  8.2 1.1 convolution_convert_fusion.4
  9.3 3.0 collective-permute-start
  12.3 3.1 collective-permute-start.1
  15.4 1.5 convolution_convert_fusion.2
  17.0 1.3 copy.33
  18.9 2.9 convolution_add_fusion
  22.8 1.4 convolution_convert_fusion.1
  24.3 20.5 %all-reduce.8.cloned.1.call-done = bf16[1024,512]{1,0:T(8,128)(2,1)} async-done(((bf16[1024,512]{1,0:T(8,128)(2,1)}), bf16[1024,512]{1,0:T(8,128)(2,1)}) %all-reduce.8.cloned.1.call-update) | async-done | bytes 1048592 | tf_op jit(solution)/shard_map/psum | solution.py:112
  44.8 1.5 convert_reduce_fusion
  46.3 1.7 fusion.12
  51.1 1.5 fusion.55
  53.0 1.9 fusion.11
  56.1 1.9 convert_reduce_fusion.1
  58.0 1.3 fusion.57
  59.3 1.8 fusion.41
  61.1 3.5 fusion.14
  65.4 184.5 %all-reduce.10.cloned.1.call-done = (f32[1536,256]{1,0:T(8,128)}, f32[256,512]{1,0:T(8,128)}, f32[1024,512]{1,0:T(8,128)}, f32[512,512]{1,0:T(8,128)}) async-done(((f32[1536,256]{1,0:T(8,128)}, f32[256,512]{1,0:T(8,128)}, f32[1024,512]{1,0:T(8,128)}, f32[512,512]{1,0:T(8,128)}), (f32[1536,256]{1,0:T(8,128)}, f32[256,512]{1,0:T(8,128)}, f32[1024,512]{1,0:T(8,128)}, ...) | async-done | bytes 5242896 | tf_op jit(solution)/shard_map/psum | solution.py:176
  249.9 1.1 copy-done.9
  251.9 4.3 %all-to-all-start = ((bf16[3,2,256,256]{3,2,0,1:T(8,128)(2,1)}), bf16[3,2,256,256]{3,2,0,1:T(8,128)(2,1)}, u32[]{:S(2)}, u32[]{:S(2)}) async-start(bf16[3,2,256,256]{3,2,0,1:T(8,128)(2,1)} %copy.35), calls=%async_computation | async-start | bytes 1572864 | tf_op jit(solution)/shard_map/all_to_all | solution.py:142
  256.3 1.6 convert_element_type.87
  258.3 2.0 copy.36
  260.3 1.1 copy.38
  261.4 19.4 %all-reduce = (f32[256]{0:T(256)S(1)}, f32[512]{0:T(512)S(1)}, f32[512]{0:T(512)S(1)}, f32[512]{0:T(512)S(1)}) all-reduce(f32[256]{0:T(256)S(1)} %copy-done.19, f32[512]{0:T(512)S(1)} %copy-done.18, f32[512]{0:T(512)S(1)} %copy-done.17, f32[512]{0:T(512)S(1)} %get-tuple-element.13), channel_id=1, replica_groups=mesh['batch'=2,'space'=8,'hidden'=2] {'space'}, use_global_device_ids=true, to_apply=%region_12.13 | all-reduce | flops 1792 | bytes 14336 | tf_op jit(solution)/shard_map/psum | solution.py:176
  280.8 6.1 %all-reduce.2 = (f32[256]{0:T(256)}, f32[512]{0:T(512)}, f32[512]{0:T(512)}, f32[512]{0:T(512)}) all-reduce(f32[256]{0:T(256)S(1)} %get-tuple-element.16, f32[512]{0:T(512)S(1)} %get-tuple-element.17, f32[512]{0:T(512)S(1)} %get-tuple-element.18, f32[512]{0:T(512)S(1)} %get-tuple-element.19), channel_id=1, replica_groups=mesh['batch'=2,'space'=8,'hidden'=2] {'batch'}, use_global_device_ids=true, to_apply=%region_13.14 | all-reduce | flops 1792 | bytes 14336 | tf_op jit(solution)/shard_map/psum | solution.py:175
  286.9 2.5 fusion.61
  289.4 1.2 fusion.59
  290.7 4.7 %collective-permute-start.3 = (bf16[1,64,256]{2,1,0:T(8,128)(2,1)S(1)}, bf16[1,64,256]{2,1,0:T(8,128)(2,1)S(1)}, u32[]{:S(2)}, u32[]{:S(2)}) collective-permute-start(bf16[1,64,256]{2,1,0:T(8,128)(2,1)S(1)} %get-tuple-element.35), channel_id=1, source_target_pairs={{2,0},{4,2},{6,4},{8,6},{10,8},{12,10},{14,12},{0,14},{3,1},{5,3},... | collective-permute-start | bytes 98312 | tf_op jit(solution)/shard_map/ppermute | solution.py:18
  296.4 1.7 fusion.16
  299.0 95.3 %all-reduce.12.cloned.1.call-done = (f32[1536,256]{1,0:T(8,128)}, f32[256,512]{1,0:T(8,128)}, f32[1024,512]{1,0:T(8,128)}, f32[512,512]{1,0:T(8,128)}) async-done(((f32[1536,256]{1,0:T(8,128)}, f32[256,512]{1,0:T(8,128)}, f32[1024,512]{1,0:T(8,128)}, f32[512,512]{1,0:T(8,128)}), (f32[1536,256]{1,0:T(8,128)}, f32[256,512]{1,0:T(8,128)}, f32[1024,512]{1,0:T(8,128)}, ...) | async-done | bytes 5242896 | tf_op jit(solution)/shard_map/psum | solution.py:175
  394.3 2.8 copy.48
  397.9 1.3 copy.50
  399.9 1.0 copy.51
  (91 shorter events, 12.9 us)
Async XLA Ops:
  7.2 41.8 %copy-start = (bf16[1024,512]{1,0:T(8,128)(2,1)S(1)}, bf16[1024,512]{1,0:T(8,128)(2,1)}, u32[]{:S(2)}) copy-start(bf16[1024,512]{1,0:T(8,128)(2,1)} %param.26) | copy-start | bytes 3145732
  7.2 11.1 %copy-start.2 = (bf16[1,128,512]{2,1,0:T(8,128)(2,1)S(1)}, bf16[1,128,512]{2,1,0:T(8,128)(2,1)}, u32[]{:S(2)}) copy-start(bf16[1,128,512]{2,1,0:T(8,128)(2,1)} %param.15) | copy-start | bytes 393220
  7.2 9.7 %copy-start.5 = (bf16[1,1024,512]{2,1,0:T(8,128)(2,1)S(1)}, bf16[1,1024,512]{2,1,0:T(8,128)(2,1)}, u32[]{:S(2)}) copy-start(bf16[1,1024,512]{2,1,0:T(8,128)(2,1)} %param.16) | copy-start | bytes 3145732
  7.2 11.1 %copy-start.13 = (s32[1024]{0:T(1024)S(1)}, s32[1024]{0:T(1024)}, u32[]{:S(2)}) copy-start(s32[1024]{0:T(1024)} %param.19) | copy-start | bytes 12292
  7.2 37.6 %all-reduce.8.cloned.1.call-start = ((), (), s32[]{:S(2)}) async-start(), calls=%async_computation.1 | async-start | bytes 2097152 | tf_op jit(solution)/shard_map/psum | solution.py:112
  9.3 9.0 %collective-permute-start = (bf16[1,64,512]{2,1,0:T(8,128)(2,1)S(1)}, bf16[1,64,512]{2,1,0:T(8,128)(2,1)S(1)}, u32[]{:S(2)}, u32[]{:S(2)}) collective-permute-start(bf16[1,64,512]{2,1,0:T(8,128)(2,1)S(1)} %get-tuple-element.36), channel_id=1, source_target_pairs={{0,2},{2,4},{4,6},{6,8},{8,10},{10,12},{12,14},{14,0},{1,3},{3,5},... | collective-permute-start | bytes 196616 | tf_op jit(solution)/shard_map/ppermute | solution.py:16
  12.3 5.9 %collective-permute-start.1 = (bf16[1,64,512]{2,1,0:T(8,128)(2,1)S(1)}, bf16[1,64,512]{2,1,0:T(8,128)(2,1)S(1)}, u32[]{:S(2)}, u32[]{:S(2)}) collective-permute-start(bf16[1,64,512]{2,1,0:T(8,128)(2,1)S(1)} %get-tuple-element.37), channel_id=1, source_target_pairs={{2,0},{4,2},{6,4},{8,6},{10,8},{12,10},{14,12},{0,14},{3,1},{5,3},... | collective-permute-start | bytes 196616 | tf_op jit(solution)/shard_map/ppermute | solution.py:18
  16.9 2.0 copy-start.22
  18.9 2.9 copy-start.23
  18.9 3.9 copy-start.21
  24.2 23.8 %copy-start.12 = (s32[1024]{0:T(1024)S(1)}, s32[1024]{0:T(1024)}, u32[]{:S(2)}) copy-start(s32[1024]{0:T(1024)} %param.20) | copy-start | bytes 12292
  24.2 23.8 %copy-start.16 = (f32[512]{0:T(512)S(1)}, f32[512]{0:T(512)}, u32[]{:S(2)}) copy-start(f32[512]{0:T(512)} %param.25) | copy-start | bytes 6148
  24.3 225.6 %all-reduce.10.cloned.1.call-start = ((), (), s32[]{:S(2)}) async-start(), calls=%async_computation.3 | async-start | bytes 10485760 | tf_op jit(solution)/shard_map/psum | solution.py:176
  44.8 3.3 copy-start.1
  46.3 2.7 copy-start.14
  48.1 1.3 copy-start.20
  51.1 1.9 copy-start.4
  53.0 1.9 copy-start.8
  54.9 1.2 copy-start.25
  59.3 1.8 copy-start.7
  64.6 222.3 %all-gather.2.cloned.1.call-start = ((), (), s32[]{:S(2)}) async-start(), calls=%async_computation.2 | async-start | bytes 1572864 | tf_op jit(solution)/shard_map/all_gather | solution.py:145
  65.4 328.9 %all-reduce.12.cloned.1.call-start = ((), (), s32[]{:S(2)}) async-start(), calls=%async_computation.4 | async-start | bytes 10485760 | tf_op jit(solution)/shard_map/psum | solution.py:175
  249.9 1.1 copy-start.9
  251.9 6.4 %all-to-all-start = ((bf16[3,2,256,256]{3,2,0,1:T(8,128)(2,1)}), bf16[3,2,256,256]{3,2,0,1:T(8,128)(2,1)}, u32[]{:S(2)}, u32[]{:S(2)}) async-start(bf16[3,2,256,256]{3,2,0,1:T(8,128)(2,1)} %copy.35), calls=%async_computation | async-start | bytes 1572864 | tf_op jit(solution)/shard_map/all_to_all | solution.py:142
  257.9 3.5 copy-start.17
  257.9 3.5 copy-start.18
  257.9 3.5 copy-start.19
  290.6 7.4 %collective-permute-start.2 = (bf16[1,64,256]{2,1,0:T(8,128)(2,1)S(1)}, bf16[1,64,256]{2,1,0:T(8,128)(2,1)S(1)}, u32[]{:S(2)}, u32[]{:S(2)}) collective-permute-start(bf16[1,64,256]{2,1,0:T(8,128)(2,1)S(1)} %get-tuple-element.34), channel_id=1, source_target_pairs={{0,2},{2,4},{4,6},{6,8},{8,10},{10,12},{12,14},{14,0},{1,3},{3,5},... | collective-permute-start | bytes 98312 | tf_op jit(solution)/shard_map/ppermute | solution.py:16
  290.7 7.4 %collective-permute-start.3 = (bf16[1,64,256]{2,1,0:T(8,128)(2,1)S(1)}, bf16[1,64,256]{2,1,0:T(8,128)(2,1)S(1)}, u32[]{:S(2)}, u32[]{:S(2)}) collective-permute-start(bf16[1,64,256]{2,1,0:T(8,128)(2,1)S(1)} %get-tuple-element.35), channel_id=1, source_target_pairs={{2,0},{4,2},{6,4},{8,6},{10,8},{12,10},{14,12},{0,14},{3,1},{5,3},... | collective-permute-start | bytes 98312 | tf_op jit(solution)/shard_map/ppermute | solution.py:18
  394.3 2.8 copy-start.11
  394.3 3.6 copy-start.3
  397.9 2.0 copy-start.6
  (3 other events, 2.8 us)
Sparse Core Ops, SparseCore 0:
  24.4 20.3 all-reduce.7
  64.7 185.0 all-reduce.9
  252.0 7.7 all-gather.1
  262.3 131.9 all-reduce.11
